TPU v7x, 64 devices: a 2x2x8 block of a 4x4x8 slice. The times are simulated.
64 devices in a mesh: rep: 4 (over x, y), pool: 16 (over z, core).
Axes of the slice: x: 2, y: 2, z: 8, core: 2. Of those that a mesh axis runs over, the one named last changes fastest.
The devices are a block of a 4x4x8 slice.
Arguments:
- kv_pool: bfloat16 [2, 4096, 2, 16, 36, 64], P(None, ('rep', 'pool')), parts along dimension 1
- page_idx: int32 [16, 64, 4], P(None, ('rep', 'pool')), parts along dimension 1
- tok_hidden: bfloat16 [64, 64, 2304], P(('rep', 'pool')), parts along dimension 0
- attn_norm: bfloat16 [2, 2304], replicated
- w_query: bfloat16 [2, 2304, 2304], replicated
- w_key: bfloat16 [2, 2304, 2304], replicated
- w_value: bfloat16 [2, 2304, 2304], replicated
- w_out: bfloat16 [2, 2304, 2304], replicated
- mlp_norm: bfloat16 [2, 2304], replicated
- w_gate: bfloat16 [2, 2304, 5760], replicated
- w_up: bfloat16 [2, 2304, 5760], replicated
- w_down: bfloat16 [2, 5760, 2304], replicated
Outputs:
- output: bfloat16 [64, 64, 2304], P(('rep', 'pool')), parts along dimension 0
There are 4 independent parts. A program takes and returns all parts, laid end to end along the dimension named above; an argument that names none is the same for every part.
All inputs are finite; a program needn't handle non-finite values.
Results may differ from a plain program's by a relative error of at most 0.0166935.
Values are sent between devices in bfloat16 or wider.
A program may use at most 768 MiB of HBM per device.

v0:
```python
import math
import jax
import jax.numpy as jnp
from jax import lax
from jax.sharding import PartitionSpec as P

NORM_EPS = 1e-6
ROPE_BASE = 10000.0


def rms_norm(vals, gain):
    vals_f = vals.astype(jnp.float32)
    inv_rms = lax.rsqrt(jnp.mean(vals_f * vals_f, axis=-1, keepdims=True) + NORM_EPS)
    return (vals_f * inv_rms * gain.astype(jnp.float32)).astype(jnp.bfloat16)


def rope_tables(offset, tokens, head_dim):
    positions = (offset + jnp.arange(tokens)).astype(jnp.float32)
    exponent = jnp.arange(head_dim // 2).astype(jnp.float32) * (-2.0 / head_dim)
    inv_freq = jnp.power(ROPE_BASE, exponent)
    angles = positions[:, None] * inv_freq[None, :]
    return jnp.cos(angles)[:, None, :], jnp.sin(angles)[:, None, :]


def apply_rope(proj, cosine, sine):
    half = proj.shape[-1] // 2
    first = proj[..., :half]
    second = proj[..., half:]
    return jnp.concatenate([first * cosine - second * sine, second * cosine + first * sine], axis=-1)


def attend(query, pages_kv, key_new, val_new):
    tokens = query.shape[-3]
    scale = 1.0 / math.sqrt(query.shape[-1])
    key_pre = pages_kv[..., :, 0, :, :, :]
    val_pre = pages_kv[..., :, 1, :, :, :]
    score_pre = jnp.einsum('...thd,...pshd->...thps', query, key_pre, preferred_element_type=jnp.float32) * scale
    score_new = jnp.einsum('...thd,...uhd->...thu', query, key_new, preferred_element_type=jnp.float32) * scale
    causal = jnp.arange(tokens)[None, :] <= jnp.arange(tokens)[:, None]
    score_new = jnp.where(causal[:, None, :], score_new, -1e30)
    row_max = jnp.maximum(jnp.max(score_pre, axis=(-2, -1)), jnp.max(score_new, axis=-1))
    exp_pre = jnp.exp(score_pre - row_max[..., None, None])
    exp_new = jnp.exp(score_new - row_max[..., None])
    row_sum = jnp.sum(exp_pre, axis=(-2, -1)) + jnp.sum(exp_new, axis=-1)
    prob_pre = (exp_pre / row_sum[..., None, None]).astype(jnp.bfloat16)
    prob_new = (exp_new / row_sum[..., None]).astype(jnp.bfloat16)
    mixed = jnp.einsum('...thps,...pshd->...thd', prob_pre, val_pre, preferred_element_type=jnp.float32)
    mixed = mixed + jnp.einsum('...thu,...uhd->...thd', prob_new, val_new, preferred_element_type=jnp.float32)
    return mixed.astype(jnp.bfloat16)


def decoder_layer(hidden, pages_kv, cosine, sine, layer_weights):
    gain_attn, q_weight, k_weight, v_weight, o_weight, gain_mlp, gate_weight, up_weight, down_weight = layer_weights
    head_shape = hidden.shape[:-1] + pages_kv.shape[-2:]
    normed = rms_norm(hidden, gain_attn)
    query = apply_rope(jnp.dot(normed, q_weight, preferred_element_type=jnp.float32).reshape(head_shape), cosine, sine).astype(jnp.bfloat16)
    key_new = apply_rope(jnp.dot(normed, k_weight, preferred_element_type=jnp.float32).reshape(head_shape), cosine, sine).astype(jnp.bfloat16)
    val_new = jnp.dot(normed, v_weight, preferred_element_type=jnp.float32).astype(jnp.bfloat16).reshape(head_shape)
    mixed = attend(query, pages_kv, key_new, val_new)
    attn_out = mixed.reshape(hidden.shape[:-1] + (q_weight.shape[1],))
    hidden = (hidden.astype(jnp.float32) + jnp.dot(attn_out, o_weight, preferred_element_type=jnp.float32)).astype(jnp.bfloat16)
    normed_mlp = rms_norm(hidden, gain_mlp)
    gate = jnp.dot(normed_mlp, gate_weight, preferred_element_type=jnp.float32)
    upper = jnp.dot(normed_mlp, up_weight, preferred_element_type=jnp.float32)
    inner = (jax.nn.silu(gate) * upper).astype(jnp.bfloat16)
    return (hidden.astype(jnp.float32) + jnp.dot(inner, down_weight, preferred_element_type=jnp.float32)).astype(jnp.bfloat16)


def solution(mesh):
    group = mesh.shape['pool']

    def local_program(kv_local, idx_local, hid_local, attn_norm, w_query, w_key, w_value, w_out, mlp_norm, w_gate, w_up, w_down):
        prefix = group * idx_local.shape[2] * kv_local.shape[3]
        cosine, sine = rope_tables(prefix, hid_local.shape[1], kv_local.shape[-1])
        page_rows = idx_local[:, 0, :].reshape(-1)
        hidden = hid_local[0]
        for layer in range(kv_local.shape[0]):
            outgoing = jnp.take(kv_local[layer], page_rows, axis=0)
            incoming = lax.all_to_all(outgoing, 'pool', 0, 0, tiled=True)
            layer_weights = (attn_norm[layer], w_query[layer], w_key[layer], w_value[layer], w_out[layer], mlp_norm[layer], w_gate[layer], w_up[layer], w_down[layer])
            hidden = decoder_layer(hidden, incoming, cosine, sine, layer_weights)
        return hidden[None]

    data_specs = (P(None, ('rep', 'pool')), P(None, ('rep', 'pool'), None), P(('rep', 'pool')))
    return jax.shard_map(local_program, mesh=mesh, in_specs=data_specs + (P(),) * 9, out_specs=P(('rep', 'pool')), check_vma=False)
```

profile of v0, /device:TPU:21, one launch (start us, length us, event | category | flops | bytes accessed | tf_op | source)
XLA Modules:
  0.0 667.0 jit_solution(5006094905379153131)
XLA Ops:
  0.0 0.8 copy.53
  0.8 0.1 reshape_squeeze.3
  0.9 26.1 %slice_bitcast_fusion = (bf16[64,2,16,36,64]{4,2,3,1,0:T(8,128)(2,1)}, bf16[64,2,16,36,64]{4,2,3,1,0:T(8,128)(2,1)}) fusion(bf16[2,64,2,16,36,64]{5,3,4,2,1,0:T(8,128)(2,1)} %param.14), kind=kLoop, calls=%fused_computation.27 | loop fusion | bytes 37748736 | tf_op jit(solution)/shard_map/squeeze | solution.py:78
  27.0 14.8 %gather_fusion.1 = bf16[64,2,16,36,64]{4,2,3,1,0:T(8,128)(2,1)} fusion(bf16[64,2,16,36,64]{4,2,3,1,0:T(8,128)(2,1)} %get-tuple-element.10, s32[1024]{0:T(1024)S(1)} %pad_clamp_fusion), kind=kCustom, calls=%fused_computation.1.clone | custom fusion | bytes 18874624 | tf_op jit(solution)/shard_map/jit(_take)/gather | solution.py:78
  41.8 14.7 %gather_fusion = bf16[64,2,16,36,64]{4,2,3,1,0:T(8,128)(2,1)} fusion(bf16[64,2,16,36,64]{4,2,3,1,0:T(8,128)(2,1)} %get-tuple-element.11, s32[1024]{0:T(1024)S(1)} %pad_clamp_fusion), kind=kCustom, calls=%fused_computation.clone | custom fusion | bytes 18874624 | tf_op jit(solution)/shard_map/jit(_take)/gather | solution.py:78
  56.5 25.0 %broadcast_select_fusion = (bf16[64,2,16,36,64]{4,2,3,1,0:T(8,128)(2,1)}, bf16[64,2,16,36,64]{4,2,3,1,0:T(8,128)(2,1)}) fusion(bf16[64,2,16,36,64]{4,2,3,1,0:T(8,128)(2,1)} %gather_fusion.1, pred[64]{0:T(512)(128)(4,1)S(1)} %compare_and_fusion, bf16[64,2,16,36,64]{4,2,3,1,0:T(8,128)(2,1)} %gather_fusion), kind=kLoop, calls=%fused_computation.30 | loop fusion | flops 9437184 | bytes 37748800 | tf_op jit(solution)/shard_map/jit(_take)/select_n | solution.py:78
  81.5 21.2 %reshape.252 = bf16[16,2,147456]{2,1,0:T(2,128)(2,1)} reshape(bf16[64,2,36,16,64]{4,3,2,1,0:T(8,128)(2,1)} %bitcast.227) | data formatting | bytes 18874368
  102.7 10.7 %all-to-all-start = ((bf16[16,2,147456]{2,1,0:T(2,128)(2,1)}), bf16[16,2,147456]{2,1,0:T(2,128)(2,1)}, u32[]{:S(2)}, u32[]{:S(2)}) async-start(bf16[16,2,147456]{2,1,0:T(2,128)(2,1)} %reshape.252), calls=%async_computation | async-start | bytes 18874368 | tf_op jit(solution)/shard_map/all_to_all | solution.py:79
  113.5 15.8 %slice_bitcast_fusion.2 = (bf16[2304,2304]{0,1:T(8,128)(2,1)}, bf16[2304,2304]{0,1:T(8,128)(2,1)}) fusion(bf16[2,2304,2304]{2,1,0:T(8,128)(2,1)} %param.19), kind=kLoop, calls=%fused_computation.44 | loop fusion | bytes 42467328 | tf_op jit(solution)/shard_map/dot_general | solution.py:57
  129.3 15.2 %copy.58 = bf16[2304,2304]{1,0:T(8,128)(2,1)} copy(bf16[2304,2304]{0,1:T(8,128)(2,1)} %get-tuple-element.13) | data formatting | bytes 21233664 | tf_op jit(solution)/shard_map/dot_general | solution.py:57
  144.5 15.7 %slice_bitcast_fusion.3 = (bf16[2304,2304]{0,1:T(8,128)(2,1)}, bf16[2304,2304]{0,1:T(8,128)(2,1)}) fusion(bf16[2,2304,2304]{2,1,0:T(8,128)(2,1)} %param.18), kind=kLoop, calls=%fused_computation.45 | loop fusion | bytes 42467328 | tf_op jit(solution)/shard_map/dot_general | solution.py:56
  160.3 15.4 %copy.56 = bf16[2304,2304]{1,0:T(8,128)(2,1)} copy(bf16[2304,2304]{0,1:T(8,128)(2,1)} %get-tuple-element.15) | data formatting | bytes 21233664 | tf_op jit(solution)/shard_map/dot_general | solution.py:56
  175.6 0.0 copy-done.7
  175.6 0.6 convert_reduce_fusion.1
  176.3 0.0 copy-done
  176.3 0.2 fusion.125
  176.4 6.0 fusion.64
  182.5 1.1 copy.88
  183.6 14.9 %copy.68 = bf16[2304,2304]{1,0:T(8,128)(2,1)} copy(bf16[2304,2304]{0,1:T(8,128)(2,1)} %get-tuple-element.12) | data formatting | bytes 21233664 | tf_op jit(solution)/shard_map/dot_general | solution.py:57
  198.5 14.9 %copy.66 = bf16[2304,2304]{1,0:T(8,128)(2,1)} copy(bf16[2304,2304]{0,1:T(8,128)(2,1)} %get-tuple-element.14) | data formatting | bytes 21233664 | tf_op jit(solution)/shard_map/dot_general | solution.py:56
  213.4 21.3 %reshape.254 = bf16[16,2,147456]{2,1,0:T(2,128)(2,1)} reshape(bf16[64,2,36,16,64]{4,3,2,1,0:T(8,128)(2,1)} %bitcast.226) | data formatting | bytes 18874368
  234.7 0.0 copy-done.8
  234.7 0.6 convert_reduce_fusion
  235.4 0.1 multiply_cosine_fusion
  235.5 0.0 copy-start.4
  235.5 5.8 fusion.144
  241.4 5.8 fusion.146
  247.2 79.0 %all-to-all-done = bf16[16,2,147456]{2,1,0:T(2,128)(2,1)} async-done(((bf16[16,2,147456]{2,1,0:T(2,128)(2,1)}), bf16[16,2,147456]{2,1,0:T(2,128)(2,1)}, u32[]{:S(2)}, u32[]{:S(2)}) %all-to-all-start) | async-done | bytes 9437216 | tf_op jit(solution)/shard_map/all_to_all | solution.py:79
  326.2 7.7 %all-to-all-start.1 = ((bf16[16,2,147456]{2,1,0:T(2,128)(2,1)}), bf16[16,2,147456]{2,1,0:T(2,128)(2,1)}, u32[]{:S(2)}, u32[]{:S(2)}) async-start(bf16[16,2,147456]{2,1,0:T(2,128)(2,1)} %reshape.254), calls=%async_computation.1 | async-start | bytes 18874368 | tf_op jit(solution)/shard_map/all_to_all | solution.py:79
  333.8 0.0 copy-done.2
  333.9 0.3 subtract_convert_fusion.2
  334.2 0.5 fusion.174
  334.7 20.6 %reshape.253 = bf16[64,2,36,16,64]{4,3,2,1,0:T(8,128)(2,1)} reshape(bf16[16,2,147456]{2,1,0:T(2,128)(2,1)} %all-to-all-done) | data formatting | bytes 18874368
  355.3 15.7 %fusion.173 = (bf16[64,1,16,36,64]{4,2,3,1,0:T(8,128)(2,1)}, bf16[64,1,16,36,64]{4,2,3,1,0:T(8,128)(2,1)}) fusion(bf16[64,2,16,36,64]{4,2,3,1,0:T(8,128)(2,1)} %bitcast.224), kind=kLoop, calls=%fused_computation.182 | loop fusion | bytes 18874368 | tf_op jit(solution)/shard_map/slice | solution.py:36
  371.0 13.6 %copy.92 = bf16[64,1,16,36,64]{0,4,2,3,1:T(8,128)(2,1)} copy(bf16[64,1,16,36,64]{4,2,3,1,0:T(8,128)(2,1)} %get-tuple-element.18) | data formatting | bytes 9437184
  384.6 12.4 %bitcast_reduce_fusion.1 = (f32[64,36]{0,1:T(8,128)S(1)}, f32[36,64,16,64]{3,1,2,0:T(8,128)}) fusion(bf16[64,36,32]{0,2,1:T(8,128)(2,1)S(1)} %get-tuple-element.30, bf16[64,36,32]{0,2,1:T(8,128)(2,1)S(1)} %get-tuple-element.31, bf16[64,1,16,36,64]{4,2,3,1,0:T(8,128)(2,1)} %get-tuple-element.19), kind=kOutput, calls=%fused_computation.24 | convolution fusion | flops 307296000 | bytes 14459904 | tf_op jit(solution)/shard_map/...thd,...pshd->...thps/dot_general | solution.py:37
  397.0 0.2 fusion.120
  397.2 10.3 %fusion.20 = f32[64,36]{0,1:T(8,128)S(1)} fusion(f32[36,64,16,64]{3,1,2,0:T(8,128)} %get-tuple-element.37, f32[64,36]{0,1:T(8,128)S(1)} %max.22), kind=kLoop, calls=%fused_computation.32 | loop fusion | flops 7075584 | bytes 9455616 | tf_op jit(solution)/shard_map/reduce_sum | solution.py:44
  407.5 12.1 %fusion.112 = f32[36,64,64]{2,1,0:T(8,128)S(1)} fusion(f32[36,64,16,64]{3,1,2,0:T(8,128)} %get-tuple-element.37, f32[64,36]{0,1:T(8,128)S(1)} %add.144, f32[64,36]{0,1:T(8,128)S(1)} %max.22, bf16[64,1,16,36,64]{0,4,2,3,1:T(8,128)(2,1)} %copy.92), kind=kOutput, calls=%fused_computation.94 | convolution fusion | flops 311427072 | bytes 14764032 | tf_op jit(solution)/shard_map/...thps,...pshd->...thd/dot_general | solution.py:47
  419.7 0.4 fusion.118
  420.0 6.1 multiply_reduce_fusion.2
  426.2 10.6 %fusion.10 = f32[64,5760]{1,0:T(8,128)S(1)} fusion(bf16[2,2304,5760]{2,1,0:T(8,128)(2,1)} %param.23, f32[64,2304]{1,0:T(8,128)S(1)} %get-tuple-element.41, f32[2304]{0:T(1024)S(1)} %get-tuple-element.7, f32[64]{0:T(128)S(1)} %add_rsqrt_fusion.2), kind=kOutput, calls=%fused_computation.12 | convolution fusion | flops 1699135488 | bytes 28615936 | tf_op jit(solution)/shard_map/dot_general | solution.py:63
  436.9 19.8 %multiply_reduce_fusion.1 = (f32[64]{0:T(128)S(1)}, f32[64,2304]{1,0:T(8,128)S(1)}) fusion(f32[64,2304]{1,0:T(8,128)S(1)} %get-tuple-element.41, bf16[2,5760,2304]{2,1,0:T(8,128)(2,1)} %param.25, bf16[2,2304,5760]{2,1,0:T(8,128)(2,1)} %param.24, f32[64,5760]{1,0:T(8,128)S(1)} %fusion.10, f32[2304]{0:T(1024)S(1)} %get-tuple-element.7, ...), kind=kOutput, calls=%fused_computation.131 | convolution fusion | flops 3400777728 | bytes 56341248 | tf_op jit(solution)/shard_map/dot_general | solution.py:66
  456.7 0.1 multiply_convert_fusion.1
  456.8 5.7 fusion.140
  462.5 5.7 fusion.142
  468.3 6.0 fusion.67
  474.2 72.3 %all-to-all-done.1 = bf16[16,2,147456]{2,1,0:T(2,128)(2,1)} async-done(((bf16[16,2,147456]{2,1,0:T(2,128)(2,1)}), bf16[16,2,147456]{2,1,0:T(2,128)(2,1)}, u32[]{:S(2)}, u32[]{:S(2)}) %all-to-all-start.1) | async-done | bytes 9437216 | tf_op jit(solution)/shard_map/all_to_all | solution.py:79
  546.6 20.8 %reshape.255 = bf16[64,2,36,16,64]{4,3,2,1,0:T(8,128)(2,1)} reshape(bf16[16,2,147456]{2,1,0:T(2,128)(2,1)} %all-to-all-done.1) | data formatting | bytes 18874368
  567.4 12.5 %fusion.172 = (bf16[64,1,16,36,64]{4,2,3,1,0:T(8,128)(2,1)}, bf16[64,1,16,36,64]{4,2,3,1,0:T(8,128)(2,1)S(1)}) fusion(bf16[64,2,16,36,64]{4,2,3,1,0:T(8,128)(2,1)} %bitcast.225), kind=kLoop, calls=%fused_computation.181 | loop fusion | bytes 18874368 | tf_op jit(solution)/shard_map/slice | solution.py:36
  579.9 0.0 copy-done.5
  579.9 0.3 subtract_convert_fusion
  580.3 11.4 %bitcast_reduce_fusion = (f32[64,36]{0,1:T(8,128)S(1)}, f32[36,64,16,64]{3,1,2,0:T(8,128)}) fusion(bf16[64,36,32]{0,2,1:T(8,128)(2,1)S(1)} %get-tuple-element.28, bf16[64,36,32]{0,2,1:T(8,128)(2,1)S(1)} %get-tuple-element.29, bf16[64,1,16,36,64]{4,2,3,1,0:T(8,128)(2,1)S(1)} %get-tuple-element.17), kind=kOutput, calls=%fused_computation.21 | convolution fusion | flops 307296000 | bytes 14459904 | tf_op jit(solution)/shard_map/...thd,...pshd->...thps/dot_general | solution.py:37
  591.7 0.5 fusion.177
  592.2 10.3 %fusion.21 = f32[64,36]{0,1:T(8,128)S(1)} fusion(f32[36,64,16,64]{3,1,2,0:T(8,128)} %get-tuple-element.45, f32[64,36]{0,1:T(8,128)S(1)} %max.23), kind=kLoop, calls=%fused_computation.33 | loop fusion | flops 7075584 | bytes 9455616 | tf_op jit(solution)/shard_map/reduce_sum | solution.py:44
  602.5 0.2 fusion.121
  602.7 13.7 %copy.94 = bf16[64,1,16,36,64]{0,4,2,3,1:T(8,128)(2,1)} copy(bf16[64,1,16,36,64]{4,2,3,1,0:T(8,128)(2,1)} %get-tuple-element.16) | data formatting | bytes 9437184
  616.4 0.3 copy.91
  616.7 12.2 %fusion.115 = f32[36,64,64]{2,1,0:T(8,128)S(1)} fusion(f32[36,64,16,64]{3,1,2,0:T(8,128)} %get-tuple-element.45, f32[64,36]{0,1:T(8,128)S(1)} %add.153, f32[64,36]{0,1:T(8,128)S(1)} %max.23, bf16[64,1,16,36,64]{0,4,2,3,1:T(8,128)(2,1)} %copy.94), kind=kOutput, calls=%fused_computation.95 | convolution fusion | flops 311427072 | bytes 14764032 | tf_op jit(solution)/shard_map/...thps,...pshd->...thd/dot_general | solution.py:47
  628.9 0.0 copy-start.9
  629.0 0.4 fusion.119
  629.3 6.2 multiply_reduce_fusion
  635.5 10.6 %fusion.4 = f32[64,5760]{1,0:T(8,128)S(1)} fusion(bf16[2,2304,5760]{2,1,0:T(8,128)(2,1)} %param.23, f32[64,2304]{1,0:T(8,128)S(1)} %get-tuple-element.49, f32[2304]{0:T(1024)S(1)} %copy-done.9, f32[64]{0:T(128)S(1)} %add_rsqrt_fusion), kind=kOutput, calls=%fused_computation.6 | convolution fusion | flops 1699135488 | bytes 28615936 | tf_op jit(solution)/shard_map/dot_general | solution.py:63
  646.2 20.4 %fusion.91 = bf16[1,64,2304]{2,1,0:T(8,128)(2,1)} fusion(f32[64,2304]{1,0:T(8,128)S(1)} %get-tuple-element.49, bf16[2,5760,2304]{2,1,0:T(8,128)(2,1)} %param.25, bf16[2,2304,5760]{2,1,0:T(8,128)(2,1)} %param.24, f32[64,5760]{1,0:T(8,128)S(1)} %fusion.4, f32[2304]{0:T(1024)S(1)} %copy-done.9, f32[64]{0:T(128)S(1)} %add_rsqrt_fusion), kind=kOutput, calls=%fused_computation.75 | convolution fusion | flops 3400335360 | bytes 56046080 | tf_op jit(solution)/shard_map/dot_general | solution.py:66
  (31 shorter events, 0.1 us)
Async XLA Ops:
  102.7 223.5 %all-to-all-start = ((bf16[16,2,147456]{2,1,0:T(2,128)(2,1)}), bf16[16,2,147456]{2,1,0:T(2,128)(2,1)}, u32[]{:S(2)}, u32[]{:S(2)}) async-start(bf16[16,2,147456]{2,1,0:T(2,128)(2,1)} %reshape.252), calls=%async_computation | async-start | bytes 18874368 | tf_op jit(solution)/shard_map/all_to_all | solution.py:79
  160.2 15.4 %copy-start.7 = (bf16[2,2304]{1,0:T(2,128)(2,1)S(1)}, bf16[2,2304]{1,0:T(2,128)(2,1)}, u32[]{:S(2)}) copy-start(bf16[2,2304]{1,0:T(2,128)(2,1)} %param.17) | copy-start | bytes 27652
  160.3 16.0 %copy-start = (bf16[1,64,2304]{2,1,0:T(8,128)(2,1)S(1)}, bf16[1,64,2304]{2,1,0:T(8,128)(2,1)}, u32[]{:S(2)}) copy-start(bf16[1,64,2304]{2,1,0:T(8,128)(2,1)} %param.16) | copy-start | bytes 884740
  213.4 21.3 %copy-start.8 = (bf16[2,2304]{1,0:T(2,128)(2,1)S(1)}, bf16[2,2304]{1,0:T(2,128)(2,1)}, u32[]{:S(2)}) copy-start(bf16[2,2304]{1,0:T(2,128)(2,1)} %param.22) | copy-start | bytes 27652
  234.7 99.4 %copy-start.10 = (pred[64,64]{0,1:T(8,128)(4,1)}, pred[64,64]{0,1:T(8,128)(4,1)S(1)}, u32[]{:S(2)}) copy-start(pred[64,64]{0,1:T(8,128)(4,1)S(1)} %iota_compare_fusion) | copy-start | bytes 12292
  235.5 98.3 %copy-start.2 = (f32[64,32]{0,1:T(8,128)}, f32[64,32]{0,1:T(8,128)S(1)}, u32[]{:S(2)}) copy-start(f32[64,32]{0,1:T(8,128)S(1)} %get-tuple-element.32) | copy-start | bytes 24580
  235.5 98.3 %copy-start.4 = (f32[64,32]{0,1:T(8,128)}, f32[64,32]{0,1:T(8,128)S(1)}, u32[]{:S(2)}) copy-start(f32[64,32]{0,1:T(8,128)S(1)} %get-tuple-element.33) | copy-start | bytes 24580
  326.2 220.4 %all-to-all-start.1 = ((bf16[16,2,147456]{2,1,0:T(2,128)(2,1)}), bf16[16,2,147456]{2,1,0:T(2,128)(2,1)}, u32[]{:S(2)}, u32[]{:S(2)}) async-start(bf16[16,2,147456]{2,1,0:T(2,128)(2,1)} %reshape.254), calls=%async_computation.1 | async-start | bytes 18874368 | tf_op jit(solution)/shard_map/all_to_all | solution.py:79
  407.5 12.1 %copy-start.1 = (bf16[64,2304]{0,1:T(8,128)(2,1)S(1)}, bf16[64,2304]{0,1:T(8,128)(2,1)}, u32[]{:S(2)}) copy-start(bf16[64,2304]{0,1:T(8,128)(2,1)} %copy.88) | copy-start | bytes 884740
  436.8 19.9 %copy-start.6 = (f32[2304]{0:T(1024)S(1)}, f32[2304]{0:T(1024)}, u32[]{:S(2)}) copy-start(f32[2304]{0:T(1024)} %get-tuple-element.8) | copy-start | bytes 27652
  567.4 12.5 %copy-start.3 = (f32[64,32]{0,1:T(8,128)S(1)}, f32[64,32]{0,1:T(8,128)}, u32[]{:S(2)}) copy-start(f32[64,32]{0,1:T(8,128)} %copy-done.2) | copy-start | bytes 24580
  567.4 12.6 %copy-start.5 = (f32[64,32]{0,1:T(8,128)S(1)}, f32[64,32]{0,1:T(8,128)}, u32[]{:S(2)}) copy-start(f32[64,32]{0,1:T(8,128)} %copy-done.4) | copy-start | bytes 24580
  580.3 11.5 %copy-start.11 = (pred[64,64]{0,1:T(8,128)(4,1)S(1)}, pred[64,64]{0,1:T(8,128)(4,1)}, u32[]{:S(2)}) copy-start(pred[64,64]{0,1:T(8,128)(4,1)} %copy-done.10) | copy-start | bytes 12292
  628.9 6.6 copy-start.9
where the time goes:
time: 680 us; the launch traced here: 667 us
  local copies, waits for them, and re-layouts  289 us (42%)
  matrix products  159 us (23%)
  waiting for transfers between devices  151 us (22%)
  other arithmetic  48.5 us (7%)
  starting transfers between devices  18.4 us (3%)
    all_to_all x2, waiting for transfers between devices, local_program(): incoming = lax.all_to_all(outgoing, 'pool', 0, 0, tiled=True)  151 us
    unnamed x31, local copies, waits for them, and re-layouts  112 us
    dot_general x3, local copies, waits for them, and re-layouts, decoder_layer(): jnp.dot(normed, q_weight, preferred_element_type=jnp.float32)  46 us
    dot_general x3, local copies, waits for them, and re-layouts, decoder_layer(): jnp.dot(normed, k_weight, preferred_element_type=jnp.float32)  46 us
    dot_general x2, matrix products, decoder_layer(): jnp.dot(inner, down_weight, preferred_element_type=jnp.float32)  40.2 us
    gather x2, local copies, waits for them, and re-layouts, local_program(): outgoing = jnp.take(kv_local[layer], page_rows, axis=0)  29.5 us
    slice x2, local copies, waits for them, and re-layouts, attend(): val_pre = pages_kv[..., :, 1, :, :, :]  28.3 us
    squeeze x1, local copies, waits for them, and re-layouts, local_program(): outgoing = jnp.take(kv_local[layer], page_rows, axis=0)  26.1 us
  transfers between devices with their start and end apart: 2, of which 2 were waited for; matrix products, arithmetic and copies ran while one was open for 41% of the time, Pallas kernels for 0%

commit v1 on v0

v1 whole, which is shorter than its diff:
```python
import functools
import jax
import jax.numpy as jnp
from jax import lax
from jax.experimental import pallas as pl
from jax.experimental.pallas import tpu as pltpu
from jax.sharding import PartitionSpec as P

NORM_EPS = 1e-6
ROPE_BASE = 10000.0
CHUNKS = 4
F32 = jnp.float32
BF16 = jnp.bfloat16


def rope_tables(offset, tokens, head_dim):
    positions = (offset + jnp.arange(tokens)).astype(F32)
    exponent = jnp.arange(head_dim // 2).astype(F32) * (-2.0 / head_dim)
    inv_freq = jnp.power(ROPE_BASE, exponent)
    angles = positions[:, None] * inv_freq[None, :]
    cosine, sine = jnp.cos(angles), jnp.sin(angles)
    return jnp.concatenate([cosine] * 4, axis=1), jnp.concatenate([-sine, sine] * 2, axis=1)


def rms_norm(vals, gain):
    vals_f = vals.astype(F32)
    inv_rms = lax.rsqrt(jnp.mean(vals_f * vals_f, axis=-1, keepdims=True) + NORM_EPS)
    return (vals_f * inv_rms * gain.astype(F32)).astype(BF16)


def pack_kernel(idx_ref, *refs):
    out_ref = refs[-1]
    pages = refs[:-1]
    page_len = pages[0].shape[4]
    pairs = out_ref.shape[2]
    for j, page in enumerate(pages):
        rows = pl.ds(j * page_len, page_len)
        for part in range(2):
            for i in range(pairs):
                both = jnp.concatenate([page[0, 0, part, 2 * i], page[0, 0, part, 2 * i + 1]], axis=-1)
                out_ref[0, part, i, rows, :] = both


def pack_pages(kv_heads, idx, layer):
    _, _, _, heads, page_len, dim = kv_heads.shape
    reqs, slots = idx.shape

    def page_spec(j):
        return pl.BlockSpec((1, 1, 2, heads, page_len, dim), lambda r, idx_ref: (layer, idx_ref[r, j], 0, 0, 0, 0))

    out_block = (1, 2, heads // 2, slots * page_len, 2 * dim)
    nbytes = kv_heads[0].size * 2
    return pl.pallas_call(
        pack_kernel,
        grid_spec=pltpu.PrefetchScalarGridSpec(
            num_scalar_prefetch=1,
            grid=(reqs,),
            in_specs=[page_spec(j) for j in range(slots)],
            out_specs=pl.BlockSpec(out_block, lambda r, idx_ref: (r, 0, 0, 0, 0)),
        ),
        out_shape=jax.ShapeDtypeStruct((reqs,) + out_block[1:], BF16),
        compiler_params=pltpu.CompilerParams(dimension_semantics=('arbitrary',)),
        cost_estimate=pl.CostEstimate(flops=0, bytes_accessed=3 * nbytes, transcendentals=0),
        name='pack_pages',
    )(idx, *([kv_heads] * slots))


def qkv_kernel(x_ref, gain_ref, cos_ref, sin_ref, wq_ref, wk_ref, wv_ref, q_ref, k_ref, v_ref, normed):
    @pl.when(pl.program_id(0) == 0)
    def _():
        normed[...] = rms_norm(x_ref[...], gain_ref[...])

    h = normed[...]
    lane = lax.broadcasted_iota(jnp.int32, cos_ref.shape, 1)
    low = (lane % 64) < 32
    cosine, sine = cos_ref[...], sin_ref[...]
    for w_ref, out_ref, rope in ((wq_ref, q_ref, True), (wk_ref, k_ref, True), (wv_ref, v_ref, False)):
        proj = jnp.dot(h, w_ref[0], preferred_element_type=F32)
        for i in range(out_ref.shape[0]):
            part = proj[:, i * 128:(i + 1) * 128]
            if rope:
                swapped = jnp.where(low, pltpu.roll(part, 96, 1), pltpu.roll(part, 32, 1))
                part = part * cosine + swapped * sine
            out_ref[i] = part.astype(BF16)


def qkv_proj(x, gain, cosine, sine, w_query, w_key, w_value, layer, tile=256):
    tokens, width = x.shape
    cols = w_query.shape[2]
    w_spec = pl.BlockSpec((1, width, tile), lambda n: (layer, 0, n))
    out_spec = pl.BlockSpec((tile // 128, tokens, 128), lambda n: (n, 0, 0))
    whole = lambda a: pl.BlockSpec(a.shape, lambda n: (0,) * a.ndim)
    out = jax.ShapeDtypeStruct((cols // 128, tokens, 128), BF16)
    return pl.pallas_call(
        qkv_kernel,
        grid=(cols // tile,),
        in_specs=[whole(x), whole(gain), whole(cosine), whole(sine), w_spec, w_spec, w_spec],
        out_specs=[out_spec] * 3,
        out_shape=[out] * 3,
        scratch_shapes=[pltpu.VMEM((tokens, width), BF16)],
        compiler_params=pltpu.CompilerParams(dimension_semantics=('arbitrary',)),
        cost_estimate=pl.CostEstimate(flops=6 * tokens * width * cols, bytes_accessed=6 * width * cols, transcendentals=0),
        name='qkv_proj',
    )(x, gain, cosine, sine, w_query, w_key, w_value)


def half_masks(shape, dtype):
    lane = lax.broadcasted_iota(jnp.int32, shape, 1)
    low = jnp.where(lane < 64, 1.0, 0.0)
    return low.astype(dtype), (1.0 - low).astype(dtype)


def block_diag(pair, low, high):
    return jnp.concatenate([pair * low, pair * high], axis=0)


def dot_t(a, b):
    return lax.dot_general(a, b, (((1,), (1,)), ((), ())), preferred_element_type=F32)


def attend_parts(query, parts, low_b, high_b, is_low, scale, masks):
    scores = []
    for (key, _), mask in zip(parts, masks):
        score = dot_t(query, block_diag(key, low_b, high_b)) * scale
        scores.append(score if mask is None else jnp.where(mask, score, -1e30))
    top0 = top1 = None
    for score in scores:
        a = jnp.max(jnp.where(is_low, score, -jnp.inf), axis=1, keepdims=True)
        b = jnp.max(jnp.where(is_low, -jnp.inf, score), axis=1, keepdims=True)
        top0 = a if top0 is None else jnp.maximum(top0, a)
        top1 = b if top1 is None else jnp.maximum(top1, b)
    top = jnp.where(is_low, top0, top1)
    sum0 = sum1 = out = None
    for score, (_, val) in zip(scores, parts):
        prob = jnp.exp(score - top)
        a = jnp.sum(jnp.where(is_low, prob, 0.0), axis=1, keepdims=True)
        b = jnp.sum(jnp.where(is_low, 0.0, prob), axis=1, keepdims=True)
        o = jnp.dot(prob.astype(BF16), block_diag(val, low_b, high_b), preferred_element_type=F32)
        sum0, sum1, out = (a, b, o) if out is None else (sum0 + a, sum1 + b, out + o)
    return out / jnp.where(is_low, sum0, sum1), (top0, top1, sum0, sum1)


def ring_kernel(group, scale, q_ref, k_ref, v_ref, kv_hbm, out_ref, kv, qbuf, obuf, loc, home, kv_sem, q_send, q_recv, o_send, o_recv):
    pairs, tokens, lanes = q_ref.shape
    half = pairs // 2
    rows = tokens // CHUNKS
    me = lax.axis_index('pool')
    right, left = lax.rem(me + 1, group), lax.rem(me + group - 1, group)
    toward = (right, left)

    barrier = pltpu.get_barrier_semaphore()
    for neighbour in toward:
        pl.semaphore_signal(barrier, inc=1, device_id={'pool': neighbour}, device_id_type=pl.DeviceIdType.MESH)
    pl.semaphore_wait(barrier, 2)

    def request_at(d, s):
        return lax.rem(me - s + group, group) if d == 0 else lax.rem(me + s, group)

    def kv_copy(d, s):
        return pltpu.make_async_copy(kv_hbm.at[request_at(d, s), :, pl.ds(half * d, half)], kv.at[d, s], kv_sem.at[d, s])

    def q_copy(d, s):
        return pltpu.make_async_remote_copy(
            src_ref=qbuf.at[d, s], dst_ref=qbuf.at[d, s + 1], send_sem=q_send.at[d, s], recv_sem=q_recv.at[d, s + 1],
            device_id={'pool': toward[d]}, device_id_type=pl.DeviceIdType.MESH)

    def q_first(d):
        return pltpu.make_async_remote_copy(
            src_ref=q_ref.at[pl.ds(half * d, half)], dst_ref=qbuf.at[d, 1], send_sem=q_send.at[d, 0], recv_sem=q_recv.at[d, 1],
            device_id={'pool': toward[d]}, device_id_type=pl.DeviceIdType.MESH)

    def o_copy(d, s, c):
        return pltpu.make_async_remote_copy(
            src_ref=obuf.at[d, s - 1, c], dst_ref=obuf.at[d, s, c], send_sem=o_send.at[d, s - 1, c], recv_sem=o_recv.at[d, s, c],
            device_id={'pool': toward[d]}, device_id_type=pl.DeviceIdType.MESH)

    for d in range(2):
        q_first(d).start()

    @pl.loop(0, group)
    def _(s):
        for d in range(2):
            kv_copy(d, s).start()

    lane = lax.broadcasted_iota(jnp.int32, (tokens, lanes), 1)
    is_low = lane < 64
    low_b, high_b = half_masks((tokens, lanes), BF16)

    def put(stat, value0, value1, j):
        return jnp.where(lane == j, value0, jnp.where(lane == 64 + j, value1, stat))

    def local_part(d, s, dest, query_at, extra):
        def one(j, carry):
            tops, sums = carry
            parts = [(kv[d, s, 0, j], kv[d, s, 1, j])] + extra[0](j)
            out, (top0, top1, sum0, sum1) = attend_parts(query_at(j), parts, low_b, high_b, is_low, scale, [None] + extra[1])
            for c in range(CHUNKS):
                dest[d, c, j] = out[c * rows:(c + 1) * rows]
            return put(tops, top0, top1, j), put(sums, sum0, sum1, j)

        zero = jnp.zeros((tokens, lanes), F32)
        tops, sums = lax.fori_loop(0, half, one, (zero, zero + 1.0), unroll=3)
        stat = tops + jnp.log(sums)
        for c in range(CHUNKS):
            dest[d, c, half] = stat[c * rows:(c + 1) * rows]

    key_at = lax.rem(lane, 64)
    causal = key_at <= lax.broadcasted_iota(jnp.int32, (tokens, lanes), 0)
    for d in range(2):
        kv_copy(d, 0).wait()
        local_part(d, 0, home, lambda j, d=d: q_ref[half * d + j],
                   (lambda j, d=d: [(k_ref[half * d + j], v_ref[half * d + j])], [causal]))

    row_low = lax.broadcasted_iota(jnp.int32, (rows, lanes), 1) < 64

    def weights(far, near):
        gap = far - near
        joint = jnp.maximum(far, near) + jnp.log(1.0 + jnp.exp(-jnp.abs(gap)))
        return 1.0 / (1.0 + jnp.exp(-gap)), joint

    def spread(stat, j):
        return jnp.where(row_low, stat[:, j:j + 1], stat[:, 64 + j:65 + j])

    def step(s, _):
        for d in range(2):
            q_copy(d, s - 1).wait_recv()

            @pl.when(s < group - 1)
            def _():
                q_copy(d, s).start()

        for d in range(2):
            kv_copy(d, s).wait()
            local_part(d, s, loc, lambda j, d=d: qbuf[d, s, j], (lambda j: [], []))

        @pl.when(s == 1)
        def _():
            for d in range(2):
                for c in range(CHUNKS):
                    obuf[d, 1, c] = loc[d, c]

        for c in range(CHUNKS):
            for d in range(2):
                @pl.when(s > 1)
                def _():
                    o_copy(d, s, c).wait_recv()
                    weight, joint = weights(obuf[d, s, c, half], loc[d, c, half])
                    for j in range(half):
                        near = loc[d, c, j]
                        obuf[d, s, c, j] = near + spread(weight, j) * (obuf[d, s, c, j] - near)
                    obuf[d, s, c, half] = joint

                o_copy(d, s + 1, c).start()
        return 0

    lax.fori_loop(1, group, step, 0)

    for c in range(CHUNKS):
        for d in range(2):
            o_copy(d, group, c).wait_recv()
            weight, _ = weights(obuf[d, group, c, half], home[d, c, half])
            for j in range(half):
                near = home[d, c, j]
                out_ref[half * d + j, c * rows:(c + 1) * rows, :] = (near + spread(weight, j) * (obuf[d, group, c, j] - near)).astype(BF16)

    for d in range(2):
        q_first(d).wait_send()

    @pl.loop(1, group)
    def _(s):
        for d in range(2):
            @pl.when(s < group - 1)
            def _():
                q_copy(d, s).wait_send()

            for c in range(CHUNKS):
                o_copy(d, s + 1, c).wait_send()


def ring_attention(query, key, val, packed, group, scale):
    pairs, tokens, lanes = query.shape
    half = pairs // 2
    rows = tokens // CHUNKS
    sem = pltpu.SemaphoreType.DMA
    vmem = pl.BlockSpec(memory_space=pltpu.VMEM)
    scratch = [
        pltpu.VMEM((2, group, 2, half, tokens, lanes), BF16),
        pltpu.VMEM((2, group, half, tokens, lanes), BF16),
        pltpu.VMEM((2, group + 1, CHUNKS, half + 1, rows, lanes), F32),
        pltpu.VMEM((2, CHUNKS, half + 1, rows, lanes), F32),
        pltpu.VMEM((2, CHUNKS, half + 1, rows, lanes), F32),
        sem((2, group)),
        sem((2, group)),
        sem((2, group)),
        sem((2, group + 1, CHUNKS)),
        sem((2, group + 1, CHUNKS)),
    ]
    return pl.pallas_call(
        functools.partial(ring_kernel, group, scale),
        out_shape=jax.ShapeDtypeStruct(query.shape, BF16),
        in_specs=[vmem, vmem, vmem, pl.BlockSpec(memory_space=pl.ANY)],
        out_specs=vmem,
        scratch_shapes=scratch,
        compiler_params=pltpu.CompilerParams(collective_id=0, has_side_effects=True),
        name='ring_attention',
    )(query, key, val, packed)


def out_kernel(x_ref, a_ref, w_ref, out_ref, rowwise):
    @pl.when(pl.program_id(0) == 0)
    def _():
        for i in range(a_ref.shape[0]):
            rowwise[:, i * 128:(i + 1) * 128] = a_ref[i]

    proj = jnp.dot(rowwise[...], w_ref[0], preferred_element_type=F32)
    out_ref[...] = (x_ref[...].astype(F32) + proj).astype(BF16)


def out_proj(x, mixed, w_out, layer, tile=256):
    tokens, width = x.shape
    depth = w_out.shape[1]
    x_spec = pl.BlockSpec((tokens, tile), lambda n: (0, n))
    return pl.pallas_call(
        out_kernel,
        grid=(width // tile,),
        in_specs=[x_spec, pl.BlockSpec(mixed.shape, lambda n: (0, 0, 0)), pl.BlockSpec((1, depth, tile), lambda n: (layer, 0, n))],
        out_specs=x_spec,
        out_shape=jax.ShapeDtypeStruct(x.shape, BF16),
        scratch_shapes=[pltpu.VMEM((tokens, depth), BF16)],
        compiler_params=pltpu.CompilerParams(dimension_semantics=('arbitrary',)),
        cost_estimate=pl.CostEstimate(flops=2 * tokens * width * depth, bytes_accessed=2 * width * depth, transcendentals=0),
        name='out_proj',
    )(x, mixed, w_out)


def mlp_kernel(x_ref, gain_ref, wg_ref, wu_ref, wd_ref, out_ref, normed, total):
    step = pl.program_id(0)

    @pl.when(step == 0)
    def _():
        normed[...] = rms_norm(x_ref[...], gain_ref[...])
        total[...] = jnp.zeros_like(total)

    h = normed[...]
    gate = jnp.dot(h, wg_ref[0], preferred_element_type=F32)
    upper = jnp.dot(h, wu_ref[0], preferred_element_type=F32)
    inner = (jax.nn.silu(gate) * upper).astype(BF16)
    total[...] += jnp.dot(inner, wd_ref[0], preferred_element_type=F32)

    @pl.when(step == pl.num_programs(0) - 1)
    def _():
        out_ref[...] = (x_ref[...].astype(F32) + total[...]).astype(BF16)


def mlp(x, gain, w_gate, w_up, w_down, layer, tile=384):
    tokens, width = x.shape
    inner = w_gate.shape[2]
    in_spec = pl.BlockSpec((1, width, tile), lambda n: (layer, 0, n))
    whole = lambda a: pl.BlockSpec(a.shape, lambda n: (0,) * a.ndim)
    return pl.pallas_call(
        mlp_kernel,
        grid=(inner // tile,),
        in_specs=[whole(x), whole(gain), in_spec, in_spec, pl.BlockSpec((1, tile, width), lambda n: (layer, n, 0))],
        out_specs=whole(x),
        out_shape=jax.ShapeDtypeStruct(x.shape, BF16),
        scratch_shapes=[pltpu.VMEM((tokens, width), BF16), pltpu.VMEM((tokens, width), F32)],
        compiler_params=pltpu.CompilerParams(dimension_semantics=('arbitrary',)),
        cost_estimate=pl.CostEstimate(flops=6 * tokens * width * inner, bytes_accessed=6 * width * inner, transcendentals=tokens * inner),
        name='mlp',
    )(x, gain, w_gate, w_up, w_down)


def solution(mesh):
    group = mesh.shape['pool']

    def local_program(kv_local, idx_local, hid_local, attn_norm, w_query, w_key, w_value, w_out, mlp_norm, w_gate, w_up, w_down):
        layers, _, _, page_len, _, dim = kv_local.shape
        prefix = group * idx_local.shape[2] * page_len
        cosine, sine = rope_tables(prefix, hid_local.shape[1], dim)
        idx = idx_local[:, 0, :]
        kv_heads = jnp.transpose(kv_local, (0, 1, 2, 4, 3, 5))
        x = hid_local[0]
        for layer in range(layers):
            packed = pack_pages(kv_heads, idx, layer)
            query, key, val = qkv_proj(x, attn_norm[layer:layer + 1], cosine, sine, w_query, w_key, w_value, layer)
            mixed = ring_attention(query, key, val, packed, group, dim ** -0.5)
            x = out_proj(x, mixed, w_out, layer)
            x = mlp(x, mlp_norm[layer:layer + 1], w_gate, w_up, w_down, layer)
        return x[None]

    data_specs = (P(None, ('rep', 'pool')), P(None, ('rep', 'pool'), None), P(('rep', 'pool')))
    return jax.shard_map(local_program, mesh=mesh, in_specs=data_specs + (P(),) * 9, out_specs=P(('rep', 'pool')), check_vma=False)
```

time: 680 us -> 393 us (0.58); the launches traced: 667 us -> 388 us
  Pallas kernels: 0 us -> 385 us
  local copies, waits for them, and re-layouts: 289 us -> 2.69 us
  matrix products: 159 us -> 0 us
  waiting for transfers between devices: 151 us -> 0 us
  other arithmetic: 48.5 us -> 0.96 us
  starting transfers between devices: 18.4 us -> 0 us
    pallas_call x0 -> x10, Pallas kernels: none -> 385 us  [the longest x2 236 us: ring_attention(): pl.pallas_call(functools.partial(ring_kernel, group, scale), out_shape=ja...]
    dot_general x20 -> x0, matrix products: 159 us -> none  [the longest x2 40.2 us: decoder_layer(): jnp.dot(inner, down_weight, preferred_element_type=jnp.float32)]
    all_to_all x2 -> x0, waiting for transfers between devices: 151 us -> none  [local_program(): incoming = lax.all_to_all(outgoing, 'pool', 0, 0, tiled=True)]
    unnamed x31 -> x4, local copies, waits for them, and re-layouts: 112 us -> 0.01 us
    dot_general x6 -> x0, local copies, waits for them, and re-layouts: 92 us -> none  [the longest x3 46 us: decoder_layer(): jnp.dot(normed, q_weight, preferred_element_type=jnp.float32)]
    gather x2 -> x0, local copies, waits for them, and re-layouts: 29.5 us -> none  [local_program(): outgoing = jnp.take(kv_local[layer], page_rows, axis=0)]
    slice x2, local copies, waits for them, and re-layouts: 28.3 us -> 2.01 us  [the longest x1 1.4 us: local_program(): attn_norm[layer:layer + 1]]
    squeeze x1, local copies, waits for them, and re-layouts: 26.1 us -> 0.68 us  [local_program(): idx = idx_local[:, 0, :]]
  transfers between devices with their start and end apart: 2 -> 0, of which waited for: 2 -> 0; matrix products, arithmetic and copies ran while one was open for 41% -> 0% of each run, Pallas kernels for 0% -> 0%
where the time goes in v1:
time: 393 us; the launch traced here: 388 us
  Pallas kernels  385 us (98%)
    pallas_call x2, Pallas kernels, ring_attention(): pl.pallas_call(functools.partial(ring_kernel, group, scale), out_shape=ja...  236 us
    pallas_call x2, Pallas kernels, mlp(): pl.pallas_call(mlp_kernel, grid=(inner // tile,), in_specs=[whole(x), who...  63.8 us
    pallas_call x2, Pallas kernels, pack_pages(): pl.pallas_call(pack_kernel, grid_spec=pltpu.PrefetchScalarGridSpec(num_sc...  34.1 us
    pallas_call x2, Pallas kernels, qkv_proj(): pl.pallas_call(qkv_kernel, grid=(cols // tile,), in_specs=[whole(x), whol...  32.1 us
    pallas_call x2, Pallas kernels, out_proj(): pl.pallas_call(out_kernel, grid=(width // tile,), in_specs=[x_spec, pl.Bl...  18.5 us

profile of v1, /device:TPU:21, one launch (start us, length us, event | category | flops | bytes accessed | tf_op | source)
XLA Modules:
  0.0 388.3 jit_solution(4331482840636698517)
XLA Ops:
  0.0 0.2 fusion
  0.2 0.7 pad_maximum_fusion
  1.0 1.4 fusion.2
  2.4 0.0 copy-start.1
  2.4 16.0 %qkv_proj.2 = (bf16[18,64,128]{2,1,0:T(8,128)(2,1)}, bf16[18,64,128]{2,1,0:T(8,128)(2,1)}, bf16[18,64,128]{2,1,0:T(8,128)(2,1)}) custom-call(bf16[64,2304]{1,0:T(8,128)(2,1)} %bitcast.12, bf16[1,2304]{1,0:T(2,128)(2,1)} %get-tuple-element.20.gain_ref, f32[64,128]{1,0:T(8,128)} %get-tuple-element.24.cos_ref, f32[64,128]{1,0:T(8,128)} %get-tuple-element.25.sin_ref, ...), custom_call_target="tpu_custom_call" | custom-call | flops 2038431744 | bytes 31850496 | tf_op jit(solution)/shard_map/qkv_proj/pallas_call | solution.py:94
  18.4 0.0 copy-done.1
  18.4 0.7 copy.13.idx_ref
  19.1 17.0 %pack_pages.2.kv_hbm = bf16[16,2,18,64,128]{4,3,2,1,0:T(8,128)(2,1)} custom-call(s32[16,4]{1,0:T(8,128)} %copy.13.idx_ref, bf16[2,64,2,36,16,64]{5,4,3,2,1,0:T(8,128)(2,1)} %bitcast.4, bf16[2,64,2,36,16,64]{5,4,3,2,1,0:T(8,128)(2,1)} %bitcast.5, bf16[2,64,2,36,16,64]{5,4,3,2,1,0:T(8,128)(2,1)} %bitcast.6, bf16[2,64,2,36,16,64]{5,4,3,2,1,0:T(8,128)(2,1)} %bitcast.7), custom_call_target="tpu_custom_call" | custom-call | bytes 28311552 | tf_op jit(solution)/shard_map/pack_pages/pallas_call | solution.py:53
  36.1 0.0 copy-start
  36.1 118.8 %ring_attention.2.a_ref = bf16[18,64,128]{2,1,0:T(8,128)(2,1)} custom-call(bf16[18,64,128]{2,1,0:T(8,128)(2,1)} %get-tuple-element.11.q_ref, bf16[18,64,128]{2,1,0:T(8,128)(2,1)} %get-tuple-element.12.k_ref, bf16[18,64,128]{2,1,0:T(8,128)(2,1)} %get-tuple-element.13.v_ref, bf16[16,2,18,64,128]{4,3,2,1,0:T(8,128)(2,1)} %pack_pages.2.kv_hbm), custom_call_target="tpu_custom_call" | custom-call | tf_op jit(solution)/shard_map/ring_attention/pallas_call | solution.py:298
  154.9 9.2 %out_proj.2.x_ref = bf16[64,2304]{1,0:T(8,128)(2,1)} custom-call(bf16[64,2304]{1,0:T(8,128)(2,1)} %bitcast.13, bf16[18,64,128]{2,1,0:T(8,128)(2,1)} %ring_attention.2.a_ref, bf16[2,2304,2304]{2,1,0:T(8,128)(2,1)} %w_ref.3), custom_call_target="tpu_custom_call" | custom-call | flops 679477248 | bytes 10616832 | tf_op jit(solution)/shard_map/out_proj/pallas_call | solution.py:323
  164.1 0.0 copy-done
  164.1 0.6 fusion.1
  164.7 32.0 %mlp.2.x_ref = bf16[64,2304]{1,0:T(8,128)(2,1)} custom-call(bf16[64,2304]{1,0:T(8,128)(2,1)} %out_proj.2.x_ref, bf16[1,2304]{1,0:T(2,128)(2,1)} %get-tuple-element.18.gain_ref, bf16[2,2304,5760]{2,1,0:T(8,128)(2,1)} %wg_ref.3, bf16[2,2304,5760]{2,1,0:T(8,128)(2,1)} %wu_ref.3, bf16[2,5760,2304]{2,1,0:T(8,128)(2,1)} %wd_ref.3), custom_call_target="tpu_custom_call" | custom-call | flops 5096079360 | bytes 79626240 | tf_op jit(solution)/shard_map/mlp/pallas_call | solution.py:360
  196.7 16.0 %qkv_proj.3 = (bf16[18,64,128]{2,1,0:T(8,128)(2,1)}, bf16[18,64,128]{2,1,0:T(8,128)(2,1)}, bf16[18,64,128]{2,1,0:T(8,128)(2,1)}) custom-call(bf16[64,2304]{1,0:T(8,128)(2,1)} %mlp.2.x_ref, bf16[1,2304]{1,0:T(2,128)(2,1)} %get-tuple-element.19.gain_ref, f32[64,128]{1,0:T(8,128)} %get-tuple-element.24.cos_ref, f32[64,128]{1,0:T(8,128)} %get-tuple-element.25.sin_ref, ...), custom_call_target="tpu_custom_call" | custom-call | flops 2038431744 | bytes 31850496 | tf_op jit(solution)/shard_map/qkv_proj/pallas_call | solution.py:94
  212.7 17.0 %pack_pages.3.kv_hbm = bf16[16,2,18,64,128]{4,3,2,1,0:T(8,128)(2,1)} custom-call(s32[16,4]{1,0:T(8,128)} %copy.13.idx_ref, bf16[2,64,2,36,16,64]{5,4,3,2,1,0:T(8,128)(2,1)} %bitcast.8, bf16[2,64,2,36,16,64]{5,4,3,2,1,0:T(8,128)(2,1)} %bitcast.9, bf16[2,64,2,36,16,64]{5,4,3,2,1,0:T(8,128)(2,1)} %bitcast.10, bf16[2,64,2,36,16,64]{5,4,3,2,1,0:T(8,128)(2,1)} %bitcast.11), custom_call_target="tpu_custom_call" | custom-call | bytes 28311552 | tf_op jit(solution)/shard_map/pack_pages/pallas_call | solution.py:53
  229.7 117.4 %ring_attention.3.a_ref = bf16[18,64,128]{2,1,0:T(8,128)(2,1)} custom-call(bf16[18,64,128]{2,1,0:T(8,128)(2,1)} %get-tuple-element.14.q_ref, bf16[18,64,128]{2,1,0:T(8,128)(2,1)} %get-tuple-element.15.k_ref, bf16[18,64,128]{2,1,0:T(8,128)(2,1)} %get-tuple-element.16.v_ref, bf16[16,2,18,64,128]{4,3,2,1,0:T(8,128)(2,1)} %pack_pages.3.kv_hbm), custom_call_target="tpu_custom_call" | custom-call | tf_op jit(solution)/shard_map/ring_attention/pallas_call | solution.py:298
  347.2 9.2 %out_proj.3.x_ref = bf16[64,2304]{1,0:T(8,128)(2,1)} custom-call(bf16[64,2304]{1,0:T(8,128)(2,1)} %mlp.2.x_ref, bf16[18,64,128]{2,1,0:T(8,128)(2,1)} %ring_attention.3.a_ref, bf16[2,2304,2304]{2,1,0:T(8,128)(2,1)} %w_ref.3), custom_call_target="tpu_custom_call" | custom-call | flops 679477248 | bytes 10616832 | tf_op jit(solution)/shard_map/out_proj/pallas_call | solution.py:323
  356.4 31.9 %mlp.3 = bf16[64,2304]{1,0:T(8,128)(2,1)} custom-call(bf16[64,2304]{1,0:T(8,128)(2,1)} %out_proj.3.x_ref, bf16[1,2304]{1,0:T(2,128)(2,1)} %get-tuple-element.17.gain_ref, bf16[2,2304,5760]{2,1,0:T(8,128)(2,1)} %wg_ref.3, bf16[2,2304,5760]{2,1,0:T(8,128)(2,1)} %wu_ref.3, bf16[2,5760,2304]{2,1,0:T(8,128)(2,1)} %wd_ref.3), custom_call_target="tpu_custom_call" | custom-call | flops 5096079360 | bytes 79626240 | tf_op jit(solution)/shard_map/mlp/pallas_call | solution.py:360
  (2 shorter events, 0.0 us)
Async XLA Ops:
  2.4 16.0 %copy-start.1 = (s32[16,1,4]{0,2,1:T(4,128)S(1)}, s32[16,1,4]{0,2,1:T(4,128)}, u32[]{:S(2)}) copy-start(s32[16,1,4]{0,2,1:T(4,128)} %param.13) | copy-start | bytes 772
  36.1 128.0 %copy-start = (bf16[2,2304]{1,0:T(2,128)(2,1)S(1)}, bf16[2,2304]{1,0:T(2,128)(2,1)}, u32[]{:S(2)}) copy-start(bf16[2,2304]{1,0:T(2,128)(2,1)} %param.20) | copy-start | bytes 27652
